TPU v7x, 32 devices: a whole 2x2x4 slice. The times are simulated.
32 devices in a mesh: gx: 4 (over z), gy: 2 (over y), gz: 4 (over x, core).
Axes of the slice: x: 2, y: 2, z: 4, core: 2. Of those that a mesh axis runs over, the one named last changes fastest.
Arguments:
- positions: float32 [3, 8, 4, 32, 128], P(None, 'gx', 'gy', 'gz'), may hold values from 0 to 1
- shield: float32 [8, 4, 32, 128], P('gx', 'gy', 'gz'), may hold values from 0.3 to 1
- width: float32 [8, 4, 32, 128], P('gx', 'gy', 'gz'), may hold values from 0.5 to 2
- hardness: float32 [8, 4, 32, 128], P('gx', 'gy', 'gz'), may hold values from 0.5 to 2
- softness: float32 [8, 4, 32, 128], P('gx', 'gy', 'gz'), may hold values from 0.5 to 2
- coupling: float32 [8, 4, 32, 128], P('gx', 'gy', 'gz'), may hold values from -0.45 to 0.45
- pair_bits: int32 [8, 4, 32], P('gx', 'gy', 'gz'), may hold values from 8192 to 134217727
- right_side: float32 [4, 8, 4, 32, 128], P(None, 'gx', 'gy', 'gz'), may hold values from -7 to 7
Outputs:
- solution: float32 [4, 8, 4, 32, 128], P(None, 'gx', 'gy', 'gz')
- residual: float32 [4, 8, 4, 32, 128], P(None, 'gx', 'gy', 'gz')
All inputs are finite; a program needn't handle non-finite values.
Results may differ from a plain program's by a relative error of at most 0.0018.
Values sent between devices are 32-bit elements; how exact they have to be, the bound alone decides.
A program may use at most 128 MiB of HBM per device.

v0:
```python
import jax
import jax.numpy as jnp
from jax import lax
from jax.sharding import PartitionSpec as P

ITERS = 3


coulomb_scale = 0.002
response_scale = 0.003


def extended(block, sides, width):
    for axis, dim in sides:
        count = lax.axis_size(axis)
        forward = [(i, i + 1) for i in range(count - 1)]
        backward = [(target, source) for source, target in forward]
        low = lax.ppermute(
            lax.slice_in_dim(block, block.shape[dim] - width, None, axis=dim), axis, forward
        )
        high = lax.ppermute(lax.slice_in_dim(block, 0, width, axis=dim), axis, backward)
        block = jnp.concatenate([low, block, high], axis=dim)
    return block


def index_tuple(values):
    return tuple((jnp.asarray(value).astype(jnp.int32) for value in values))


def pair_terms(own_params, partner, offset_code, own_bits):
    shift_first = (offset_code // 9 - 1).astype(jnp.float32)
    shift_second = (offset_code // 3 % 3 - 1).astype(jnp.float32)
    shift_third = (offset_code % 3 - 1).astype(jnp.float32)

    def separation(column, shift):
        return shift + (partner[column][:, None, :] - own_params[column][:, :, None])

    first = separation(0, shift_first)
    second = separation(1, shift_second)
    third = separation(2, shift_third)
    distance = first * first + second * second + third * third
    coulomb = coulomb_scale * lax.rsqrt(
        distance + own_params[3][:, :, None] * partner[3][:, None, :]
    )
    response = response_scale * jnp.exp(
        -distance / (own_params[4][:, :, None] + partner[4][:, None, :])
    )
    listed = jnp.right_shift(own_bits, offset_code) & 1 > 0
    tile_size = own_params.shape[2]
    diagonal_mask = lax.broadcasted_iota(
        jnp.int32, (tile_size, tile_size), 0
    ) == lax.broadcasted_iota(jnp.int32, (tile_size, tile_size), 1)
    kept = listed[:, None, None] & jnp.logical_not(diagonal_mask[None] & (offset_code == 13))
    empty_pair = jnp.zeros_like(distance)
    return (
        jnp.where(kept, coulomb, empty_pair).astype(jnp.bfloat16),
        jnp.where(kept, response, empty_pair).astype(jnp.bfloat16),
    )


def tile_block(padded, offset_code, extent):
    fields = padded.shape[0]
    tile_size = padded.shape[4]
    start = index_tuple((0, offset_code // 9, offset_code // 3 % 3, offset_code % 3, 0))
    block = lax.dynamic_slice(padded, start, (fields, extent[0], extent[1], extent[2], tile_size))
    return block.reshape(fields, extent[0] * extent[1] * extent[2], tile_size)


def static_block(padded, offset_code, extent):
    first = offset_code // 9
    second = offset_code // 3 % 3
    third = offset_code % 3
    block = padded[
        :, first : first + extent[0], second : second + extent[1], third : third + extent[2]
    ]
    return block.reshape(padded.shape[0], extent[0] * extent[1] * extent[2], padded.shape[4])


def spread_ghosts(vector, extent):
    shaped = vector.reshape(4, extent[0], extent[1], extent[2], vector.shape[2])
    return extended(shaped, (("gx", 1), ("gy", 2), ("gz", 3)), 1)


def split_parts(padded):
    upper = padded.astype(jnp.bfloat16)
    lower = (padded - upper.astype(jnp.float32)).astype(jnp.bfloat16)
    return jnp.concatenate([upper[:2], lower[:2], upper[2:], lower[2:]], axis=0)


def inner_local(vector, other_vector):
    return jnp.sum((vector * other_vector).reshape(2, 2, -1), axis=(0, 2))


def two_products(vector, applied):
    return lax.psum((inner_local(vector, vector), inner_local(vector, applied)), ("gx", "gy", "gz"))


def widen(scalars):
    return jnp.concatenate([scalars, scalars]).reshape(4, 1, 1)


def on_device(positions, shield, width, hardness, softness, coupling, pair_bits, right_side):
    tiles_x, tiles_y, tiles_z, tile_size = hardness.shape
    extent = (tiles_x, tiles_y, tiles_z)
    tile_count = tiles_x * tiles_y * tiles_z
    params = jnp.concatenate([positions, shield[None], width[None]], axis=0)
    joined = extended(
        jnp.concatenate([params, right_side], axis=0), (("gx", 1), ("gy", 2), ("gz", 3)), 1
    )
    params_pad = joined[:5]
    first_pad = joined[5:]
    own_params = params_pad[:, 1:-1, 1:-1, 1:-1].reshape(5, tile_count, tile_size)
    own_bits = pair_bits.reshape(tile_count)

    def build(offset_code, carry):
        store_coulomb, store_response, row_coulomb, row_response = carry
        offset_code = offset_code.astype(jnp.int32)
        partner = tile_block(params_pad, offset_code, extent)
        coulomb, response = pair_terms(own_params, partner, offset_code, own_bits)
        store_coulomb = lax.dynamic_update_index_in_dim(store_coulomb, coulomb, offset_code, 0)
        store_response = lax.dynamic_update_index_in_dim(store_response, response, offset_code, 0)
        row_coulomb = row_coulomb + jnp.sum(coulomb.astype(jnp.float32), axis=2)
        row_response = row_response + jnp.sum(response.astype(jnp.float32), axis=2)
        return (store_coulomb, store_response, row_coulomb, row_response)

    store_zeros = jnp.zeros((27, tile_count, tile_size, tile_size), jnp.bfloat16)
    flat_zeros = jnp.zeros((tile_count, tile_size), jnp.float32)
    store_coulomb, store_response, row_coulomb, row_response = lax.fori_loop(
        0, 27, build, (store_zeros, store_zeros, flat_zeros, flat_zeros)
    )
    diagonal_charge = hardness.reshape(tile_count, tile_size) + row_coulomb
    diagonal_potential = softness.reshape(tile_count, tile_size) + row_response
    linking = coupling.reshape(tile_count, tile_size)

    def operate(padded, vector):
        parts_pad = split_parts(padded)
        stacked = jnp.stack(
            [static_block(parts_pad, offset_code, extent) for offset_code in range(27)], axis=0
        )
        charge_terms = jnp.einsum(
            "otij,oftj->fti", store_coulomb, stacked[:, :4], preferred_element_type=jnp.float32
        )
        potential_terms = jnp.einsum(
            "otij,oftj->fti", store_response, stacked[:, 4:], preferred_element_type=jnp.float32
        )
        pair_charge = charge_terms[:2] + charge_terms[2:]
        pair_potential = potential_terms[:2] + potential_terms[2:]
        image_charge = diagonal_charge * vector[:2] + pair_charge + linking * vector[2:]
        image_potential = diagonal_potential * vector[2:] - pair_potential + linking * vector[:2]
        return jnp.concatenate([image_charge, image_potential], axis=0)

    rhs_flat = right_side.reshape(4, tile_count, tile_size)
    solution = jnp.zeros_like(rhs_flat)
    applied = operate(first_pad, rhs_flat)
    norm_now, product = two_products(rhs_flat, applied)
    step_size = norm_now / product
    remainder = rhs_flat
    direction = rhs_flat
    along = applied
    for iteration in range(ITERS):
        solution = solution + widen(step_size) * direction
        remainder = remainder - widen(step_size) * along
        if iteration + 1 < ITERS:
            applied = operate(spread_ghosts(remainder, extent), remainder)
            norm_next, product = two_products(remainder, applied)
            beta_ratio = norm_next / norm_now
            step_size = norm_next / (product - beta_ratio * norm_next / step_size)
            direction = remainder + widen(beta_ratio) * direction
            along = applied + widen(beta_ratio) * along
            norm_now = norm_next
    final_image = operate(spread_ghosts(solution, extent), solution)
    residual = rhs_flat - final_image
    shape_out = (4, tiles_x, tiles_y, tiles_z, tile_size)
    return (solution.reshape(shape_out), residual.reshape(shape_out))


def solution(mesh):
    return jax.shard_map(
        on_device,
        mesh=mesh,
        in_specs=(
            P(None, "gx", "gy", "gz", None),
            P("gx", "gy", "gz", None),
            P("gx", "gy", "gz", None),
            P("gx", "gy", "gz", None),
            P("gx", "gy", "gz", None),
            P("gx", "gy", "gz", None),
            P("gx", "gy", "gz"),
            P(None, "gx", "gy", "gz", None),
        ),
        out_specs=(P(None, "gx", "gy", "gz", None), P(None, "gx", "gy", "gz", None)),
        check_vma=False,
    )
```

profile of v0, /device:TPU:0, one launch (start us, length us, event | category | flops | bytes accessed | tf_op | source)
XLA Modules:
  0.0 624.8 jit_solution(3941174055811860574)
XLA Ops:
  2.9 5.6 collective-permute-start
  27.8 282.4 %while.23 = (s32[]{:T(128)}, bf16[27,32,128,128]{3,2,0,1:T(8,128)(2,1)}, bf16[27,32,128,128]{3,2,0,1:T(8,128)(2,1)}, f32[32,128]{1,0:T(8,128)S(1)}, f32[32,128]{...) while((s32[]{:T(128)}, ...), condition=%wide.region_6.7_spmd.clone, body=%wide.region_3.6_spmd.clone.sunk | while | flops 26271884 | bytes 2933673 | solution.py:128
  27.9 5.2 fusion.83
  33.2 5.0 convert_reduce_fusion.3
  38.4 5.2 fusion.83
  43.6 5.0 convert_reduce_fusion.3
  48.9 5.2 fusion.83
  54.1 5.0 convert_reduce_fusion.3
  59.4 5.2 fusion.83
  64.6 5.0 convert_reduce_fusion.3
  69.9 5.2 fusion.83
  75.1 5.0 convert_reduce_fusion.3
  80.3 5.3 fusion.83
  85.6 5.0 convert_reduce_fusion.3
  90.8 5.2 fusion.83
  96.0 5.0 convert_reduce_fusion.3
  101.3 5.2 fusion.83
  106.5 5.0 convert_reduce_fusion.3
  111.7 5.2 fusion.83
  116.9 5.0 convert_reduce_fusion.3
  122.2 5.2 fusion.83
  127.4 5.0 convert_reduce_fusion.3
  132.6 5.2 fusion.83
  137.8 5.0 convert_reduce_fusion.3
  143.1 5.2 fusion.83
  148.3 5.0 convert_reduce_fusion.3
  153.5 5.2 fusion.83
  158.7 5.0 convert_reduce_fusion.3
  164.0 5.2 fusion.83
  169.2 5.0 convert_reduce_fusion.3
  174.4 5.2 fusion.83
  179.6 5.0 convert_reduce_fusion.3
  184.8 5.2 fusion.83
  190.1 5.0 convert_reduce_fusion.3
  195.3 5.2 fusion.83
  200.5 5.0 convert_reduce_fusion.3
  205.8 5.2 fusion.83
  211.0 5.0 convert_reduce_fusion.3
  216.2 5.2 fusion.83
  221.4 5.0 convert_reduce_fusion.3
  226.7 5.2 fusion.83
  231.9 5.0 convert_reduce_fusion.3
  237.1 5.3 fusion.83
  242.4 5.0 convert_reduce_fusion.3
  247.6 5.3 fusion.83
  252.9 5.0 convert_reduce_fusion.3
  258.1 5.2 fusion.83
  263.4 5.0 convert_reduce_fusion.3
  268.6 5.2 fusion.83
  279.1 5.2 fusion.83
  289.5 5.2 fusion.83
  299.9 5.2 fusion.83
  305.1 5.0 convert_reduce_fusion.3
  312.6 13.1 %convolution_bitcast_fusion.6 = f32[4,32,128]{2,0,1:T(4,128)S(1)} fusion(bf16[27,32,128,128]{3,2,0,1:T(8,128)(2,1)} %get-tuple-element.243, bf16[27,8,32,128]{3,1,0,2:T(8,128)(2,1)S(1)} %constant_dynamic-update-slice_fusion), kind=kOutput, calls=%fused_computation.39 | convolution fusion | flops 113246208 | bytes 29261824 | tf_op jit(solution)/shard_map/otij,oftj->fti/dot_general | solution.py:143
  325.7 13.4 %convolution_bitcast_fusion.7 = f32[4,32,128]{2,0,1:T(4,128)S(1)} fusion(bf16[27,32,128,128]{3,2,0,1:T(8,128)(2,1)} %get-tuple-element.241, bf16[27,8,32,128]{3,1,0,2:T(8,128)(2,1)S(1)} %constant_dynamic-update-slice_fusion), kind=kOutput, calls=%fused_computation.40 | convolution fusion | flops 113246208 | bytes 29261824 | tf_op jit(solution)/shard_map/otij,oftj->fti/dot_general | solution.py:140
  339.6 45.1 %all-reduce.2 = (f32[2]{0:T(128)S(1)}, f32[2]{0:T(128)S(1)}) all-reduce(f32[2]{0:T(128)S(1)} %reduce_sum.132, f32[2]{0:T(128)S(1)} %reduce_sum.135), channel_id=1, replica_groups=mesh['gx'=4,'gy'=2,'gz'=4] {'gx','gy','gz'}, use_global_device_ids=true, to_apply=%region_2.3 | all-reduce | flops 4 | bytes 32 | tf_op jit(solution)/shard_map/psum | solution.py:95
  407.9 13.1 %convolution_bitcast_fusion.4 = f32[4,32,128]{2,0,1:T(4,128)S(1)} fusion(bf16[27,32,128,128]{3,2,0,1:T(8,128)(2,1)} %get-tuple-element.243, bf16[27,8,32,128]{3,1,0,2:T(8,128)(2,1)S(1)} %constant_dynamic-update-slice_fusion.29), kind=kOutput, calls=%fused_computation.37 | convolution fusion | flops 113246208 | bytes 29261824 | tf_op jit(solution)/shard_map/otij,oftj->fti/dot_general | solution.py:143
  420.9 13.4 %convolution_bitcast_fusion.5 = f32[4,32,128]{2,0,1:T(4,128)S(1)} fusion(bf16[27,32,128,128]{3,2,0,1:T(8,128)(2,1)} %get-tuple-element.241, bf16[27,8,32,128]{3,1,0,2:T(8,128)(2,1)S(1)} %constant_dynamic-update-slice_fusion.29), kind=kOutput, calls=%fused_computation.38 | convolution fusion | flops 113246208 | bytes 29261824 | tf_op jit(solution)/shard_map/otij,oftj->fti/dot_general | solution.py:140
  434.7 44.7 %all-reduce.1 = (f32[2]{0:T(128)S(1)}, f32[2]{0:T(128)S(1)}) all-reduce(f32[2]{0:T(128)S(1)} %reduce_sum.138, f32[2]{0:T(128)S(1)} %reduce_sum.141), channel_id=1, replica_groups=mesh['gx'=4,'gy'=2,'gz'=4] {'gx','gy','gz'}, use_global_device_ids=true, to_apply=%region_12.13 | all-reduce | flops 4 | bytes 32 | tf_op jit(solution)/shard_map/psum | solution.py:95
  502.8 13.4 %convolution_bitcast_fusion.3 = f32[4,32,128]{2,0,1:T(4,128)S(1)} fusion(bf16[27,32,128,128]{3,2,0,1:T(8,128)(2,1)} %get-tuple-element.241, bf16[27,8,32,128]{3,1,0,2:T(8,128)(2,1)S(1)} %constant_dynamic-update-slice_fusion.58), kind=kOutput, calls=%fused_computation.36 | convolution fusion | flops 113246208 | bytes 29261824 | tf_op jit(solution)/shard_map/otij,oftj->fti/dot_general | solution.py:140
  516.1 13.1 %convolution_bitcast_fusion.2 = f32[4,32,128]{2,0,1:T(4,128)S(1)} fusion(bf16[27,32,128,128]{3,2,0,1:T(8,128)(2,1)} %get-tuple-element.243, bf16[27,8,32,128]{3,1,0,2:T(8,128)(2,1)S(1)} %constant_dynamic-update-slice_fusion.58), kind=kOutput, calls=%fused_computation.35 | convolution fusion | flops 113246208 | bytes 29261824 | tf_op jit(solution)/shard_map/otij,oftj->fti/dot_general | solution.py:143
  529.6 44.8 %all-reduce = (f32[2]{0:T(128)S(1)}, f32[2]{0:T(128)S(1)}) all-reduce(f32[2]{0:T(128)S(1)} %reduce_sum.144, f32[2]{0:T(128)S(1)} %reduce_sum.147), channel_id=1, replica_groups=mesh['gx'=4,'gy'=2,'gz'=4] {'gx','gy','gz'}, use_global_device_ids=true, to_apply=%region_18.19 | all-reduce | flops 4 | bytes 32 | tf_op jit(solution)/shard_map/psum | solution.py:95
  597.5 13.4 %convolution_bitcast_fusion.1 = f32[4,32,128]{2,0,1:T(4,128)S(1)} fusion(bf16[27,32,128,128]{3,2,0,1:T(8,128)(2,1)} %get-tuple-element.241, bf16[27,8,32,128]{3,1,0,2:T(8,128)(2,1)S(1)} %constant_dynamic-update-slice_fusion.85), kind=kOutput, calls=%fused_computation.34 | convolution fusion | flops 113246208 | bytes 29261824 | tf_op jit(solution)/shard_map/otij,oftj->fti/dot_general | solution.py:140
  610.9 13.1 %convolution_bitcast_fusion = f32[4,32,128]{2,0,1:T(4,128)S(1)} fusion(bf16[27,32,128,128]{3,2,0,1:T(8,128)(2,1)} %get-tuple-element.243, bf16[27,8,32,128]{3,1,0,2:T(8,128)(2,1)S(1)} %constant_dynamic-update-slice_fusion.85), kind=kOutput, calls=%fused_computation.33 | convolution fusion | flops 113246208 | bytes 29261824 | tf_op jit(solution)/shard_map/otij,oftj->fti/dot_general | solution.py:143
  (522 shorter events, 110.8 us)
Async XLA Ops:
  0.6 16.6 %copy-start = (f32[4,2,2,8,128]{4,3,2,1,0:T(8,128)S(1)}, f32[4,2,2,8,128]{4,3,2,1,0:T(8,128)}, u32[]{:S(2)}) copy-start(f32[4,2,2,8,128]{4,3,2,1,0:T(8,128)} %param.17) | copy-start | bytes 196612
  0.6 19.3 %copy-start.4 = (f32[2,2,8,128]{3,2,1,0:T(8,128)S(1)}, f32[2,2,8,128]{3,2,1,0:T(8,128)}, u32[]{:S(2)}) copy-start(f32[2,2,8,128]{3,2,1,0:T(8,128)} %param.12) | copy-start | bytes 49156
  0.7 19.3 %copy-start.5 = (f32[2,2,8,128]{3,2,1,0:T(8,128)S(1)}, f32[2,2,8,128]{3,2,1,0:T(8,128)}, u32[]{:S(2)}) copy-start(f32[2,2,8,128]{3,2,1,0:T(8,128)} %param.11) | copy-start | bytes 49156
  0.7 19.3 %copy-start.3 = (f32[3,2,2,8,128]{4,3,2,1,0:T(8,128)S(1)}, f32[3,2,2,8,128]{4,3,2,1,0:T(8,128)}, u32[]{:S(2)}) copy-start(f32[3,2,2,8,128]{4,3,2,1,0:T(8,128)} %param.10) | copy-start | bytes 147460
  1.6 7.7 %collective-permute-start.1 = (f32[9,1,2,8,128]{4,3,2,1,0:T(8,128)S(1)}, f32[9,1,2,8,128]{4,3,2,1,0:T(8,128)S(1)}, u32[]{:S(2)}, u32[]{:S(2)}) collective-permute-start(f32[9,1,2,8,128]{4,3,2,1,0:T(8,128)S(1)} %get-tuple-element.453), channel_id=1, source_target_pairs={{8,0},{16,8},{24,16},{9,1},{17,9},{25,17},{10,2},{18,10},{26,18},{... | collective-permute-start | bytes 221192 | tf_op jit(solution)/shard_map/ppermute | solution.py:21
  2.9 7.6 %collective-permute-start = (f32[9,1,2,8,128]{4,3,2,1,0:T(8,128)S(1)}, f32[9,1,2,8,128]{4,3,2,1,0:T(8,128)S(1)}, u32[]{:S(2)}, u32[]{:S(2)}) collective-permute-start(f32[9,1,2,8,128]{4,3,2,1,0:T(8,128)S(1)} %get-tuple-element.452), channel_id=1, source_target_pairs={{0,8},{8,16},{16,24},{1,9},{9,17},{17,25},{2,10},{10,18},{18,26},{... | collective-permute-start | bytes 221192 | tf_op jit(solution)/shard_map/ppermute | solution.py:18
  11.4 7.0 %collective-permute-start.3 = (f32[9,4,1,8,128]{4,3,2,1,0:T(8,128)S(1)}, f32[9,4,1,8,128]{4,3,2,1,0:T(8,128)S(1)}, u32[]{:S(2)}, u32[]{:S(2)}) collective-permute-start(f32[9,4,1,8,128]{4,3,2,1,0:T(8,128)S(1)} %get-tuple-element.429), channel_id=1, source_target_pairs={{4,0},{5,1},{6,2},{7,3},{12,8},{13,9},{14,10},{15,11},{20,16},{21,... | collective-permute-start | bytes 442376 | tf_op jit(solution)/shard_map/ppermute | solution.py:21
  12.7 7.2 %collective-permute-start.2 = (f32[9,4,1,8,128]{4,3,2,1,0:T(8,128)S(1)}, f32[9,4,1,8,128]{4,3,2,1,0:T(8,128)S(1)}, u32[]{:S(2)}, u32[]{:S(2)}) collective-permute-start(f32[9,4,1,8,128]{4,3,2,1,0:T(8,128)S(1)} %get-tuple-element.428), channel_id=1, source_target_pairs={{0,4},{1,5},{2,6},{3,7},{8,12},{9,13},{10,14},{11,15},{16,20},{17,... | collective-permute-start | bytes 442376 | tf_op jit(solution)/shard_map/ppermute | solution.py:18
  20.1 4.4 collective-permute-start.5
  21.4 3.9 collective-permute-start.4
  25.5 1.0 copy-start.1
  26.7 1.1 slice-start
  325.7 13.4 %copy-start.8 = (f32[2,2,8,128]{3,2,1,0:T(8,128)S(1)}, f32[2,2,8,128]{3,2,1,0:T(8,128)}, u32[]{:S(2)}) copy-start(f32[2,2,8,128]{3,2,1,0:T(8,128)} %param.14) | copy-start | bytes 49156
  325.7 13.4 %copy-start.9 = (f32[2,2,8,128]{3,2,1,0:T(8,128)S(1)}, f32[2,2,8,128]{3,2,1,0:T(8,128)}, u32[]{:S(2)}) copy-start(f32[2,2,8,128]{3,2,1,0:T(8,128)} %param.13) | copy-start | bytes 49156
  325.7 13.4 %copy-start.6 = (f32[2,2,8,128]{3,2,1,0:T(8,128)S(1)}, f32[2,2,8,128]{3,2,1,0:T(8,128)}, u32[]{:S(2)}) copy-start(f32[2,2,8,128]{3,2,1,0:T(8,128)} %param.15) | copy-start | bytes 49156
  325.7 13.4 %copy-start.7 = (f32[2,2,2,8,128]{4,0,3,2,1:T(2,128)S(1)}, f32[2,2,2,8,128]{4,0,3,2,1:T(2,128)}, u32[]{:S(2)}) copy-start(f32[2,2,2,8,128]{4,0,3,2,1:T(2,128)} %copy.141) | copy-start | bytes 98308
  385.0 5.9 collective-permute-start.7
  386.3 6.1 collective-permute-start.6
  392.4 6.2 collective-permute-start.9
  393.7 6.4 %collective-permute-start.8 = (f32[4,4,1,8,128]{4,3,2,1,0:T(8,128)S(1)}, f32[4,4,1,8,128]{4,3,2,1,0:T(8,128)S(1)}, u32[]{:S(2)}, u32[]{:S(2)}) collective-permute-start(f32[4,4,1,8,128]{4,3,2,1,0:T(8,128)S(1)} %get-tuple-element.458), channel_id=1, source_target_pairs={{0,4},{1,5},{2,6},{3,7},{8,12},{9,13},{10,14},{11,15},{16,20},{17,... | collective-permute-start | bytes 196616 | tf_op jit(solution)/shard_map/ppermute | solution.py:18
  400.2 4.7 collective-permute-start.11
  401.5 3.9 collective-permute-start.10
  479.9 5.9 collective-permute-start.13
  481.2 6.1 collective-permute-start.12
  487.3 6.2 collective-permute-start.15
  488.6 6.4 %collective-permute-start.14 = (f32[4,4,1,8,128]{4,3,2,1,0:T(8,128)S(1)}, f32[4,4,1,8,128]{4,3,2,1,0:T(8,128)S(1)}, u32[]{:S(2)}, u32[]{:S(2)}) collective-permute-start(f32[4,4,1,8,128]{4,3,2,1,0:T(8,128)S(1)} %get-tuple-element.456), channel_id=1, source_target_pairs={{0,4},{1,5},{2,6},{3,7},{8,12},{9,13},{10,14},{11,15},{16,20},{17,... | collective-permute-start | bytes 196616 | tf_op jit(solution)/shard_map/ppermute | solution.py:18
  495.1 4.4 collective-permute-start.17
  496.4 3.9 collective-permute-start.16
  574.6 20.9 %copy-start.2 = (f32[4,2,2,8,128]{4,3,2,1,0:T(8,128)}, f32[4,2,2,8,128]{4,3,2,1,0:T(8,128)S(1)}, u32[]{:S(2)}) copy-start(f32[4,2,2,8,128]{4,3,2,1,0:T(8,128)S(1)} %multiply_add_fusion.2) | copy-start | bytes 196612
  574.7 5.9 collective-permute-start.19
  576.0 6.1 collective-permute-start.18
  582.1 6.2 collective-permute-start.21
  583.4 6.4 %collective-permute-start.20 = (f32[4,4,1,8,128]{4,3,2,1,0:T(8,128)S(1)}, f32[4,4,1,8,128]{4,3,2,1,0:T(8,128)S(1)}, u32[]{:S(2)}, u32[]{:S(2)}) collective-permute-start(f32[4,4,1,8,128]{4,3,2,1,0:T(8,128)S(1)} %get-tuple-element.454), channel_id=1, source_target_pairs={{0,4},{1,5},{2,6},{3,7},{8,12},{9,13},{10,14},{11,15},{16,20},{17,... | collective-permute-start | bytes 196616 | tf_op jit(solution)/shard_map/ppermute | solution.py:18
  589.9 4.5 collective-permute-start.23
  591.2 3.9 collective-permute-start.22
where the time goes:
time: 629 us; the launch traced here: 625 us
  other arithmetic  283 us (45%)
  blocking collectives  135 us (21%)
  matrix products  106 us (17%)
  starting transfers between devices  65.2 us (10%)
  waiting for transfers between devices  16.2 us (3%)
  local copies, waits for them, and re-layouts  12.7 us (2%)
    dynamic_update_slice x27, other arithmetic, build(): lax.dynamic_update_index_in_dim(store_response, response, offset_code, 0)  141 us
    reduce_sum x27, other arithmetic, build(): row_response = row_response + jnp.sum(response.astype(jnp.float32), axis=2)  135 us
    psum x3, blocking collectives, two_products(): lax.psum((inner_local(vector, vector), inner_local(vector, applied)), ('g...  135 us
    dot_general x4, matrix products, operate(): jnp.einsum('otij,oftj->fti', store_coulomb, stacked[:, :4], preferred_ele...  53.5 us
    dot_general x4, matrix products, operate(): jnp.einsum('otij,oftj->fti', store_response, stacked[:, 4:], preferred_el...  52.3 us
    ppermute x12, starting transfers between devices, extended(): lax.ppermute(lax.slice_in_dim(block, block.shape[dim] - width, None, axis...  49.7 us
    ppermute x12, starting transfers between devices, extended(): lax.ppermute(lax.slice_in_dim(block, 0, width, axis=dim), axis, backward)  15.5 us
    ppermute x12, waiting for transfers between devices, extended(): lax.ppermute(lax.slice_in_dim(block, block.shape[dim] - width, None, axis...  14.9 us
  transfers between devices with their start and end apart: 24, of which 16 were waited for; matrix products, arithmetic and copies ran while one was open for 0% of the time, Pallas kernels for 0%

commit v1 on v0

v1 whole, which is shorter than its diff:
```python
import functools
import itertools

import jax
import jax.numpy as jnp
from jax import lax
from jax.experimental import pallas as pl
from jax.experimental.pallas import tpu as pltpu
from jax.sharding import PartitionSpec as P

ITERS = 3
AXES = ("gx", "gy", "gz")
DIRECTIONS = [d for d in itertools.product((-1, 0, 1), repeat=3) if d != (0, 0, 0)]

coulomb_scale = 0.002
response_scale = 0.003


def sides(step, count, unit):
    if step < 0:
        return pl.ds(unit, unit), pl.ds((count + 1) * unit, unit)
    if step > 0:
        return pl.ds(count * unit, unit), pl.ds(0, unit)
    return pl.ds(unit, count * unit), pl.ds(unit, count * unit)


def kernel(
    counts, extent, tile,
    bits_ref, params_ref, rhs_ref, aux_ref, sol_ref, res_ref,
    store, param_pad, rem_pad, along_pad, ghosts, lhs, columns, diag, direction, sums, parts,
    halo_send, halo_recv, sum_send, sum_recv,
):
    tx, ty, tz = extent
    me = [lax.axis_index(axis) for axis in AXES]

    def exists(d):
        ok = None
        for m, step, count in zip(me, d, counts):
            if step:
                here = (m + step >= 0) & (m + step < count)
                ok = here if ok is None else ok & here
        return ok

    def halo_copy(ref, slot, index, d):
        pairs = [sides(s, n, u) for s, n, u in zip(d, extent, (1, 1, tile))]
        source = (pairs[0][0], pairs[1][0], slice(None), pairs[2][0])
        target = (pairs[0][1], pairs[1][1], slice(None), pairs[2][1])
        return pltpu.make_async_remote_copy(
            src_ref=ref.at[source],
            dst_ref=ref.at[target],
            send_sem=halo_send.at[slot, index],
            recv_sem=halo_recv.at[slot, index],
            device_id=tuple(m + s for m, s in zip(me, d)),
            device_id_type=pl.DeviceIdType.MESH,
        )

    def halo_start(ref, slot, fill):
        for index, d in enumerate(DIRECTIONS):
            there = exists(d)

            @pl.when(there)
            def _():
                halo_copy(ref, slot, index, d).start()

            back = tuple(-s for s in d)
            strips = [sides(s, n, u)[1] for s, n, u in zip(back, extent, (1, 1, tile))]

            @pl.when(jnp.logical_not(there))
            def _():
                region = (strips[0], strips[1], slice(None), strips[2])
                ref[region] = jnp.full(ref.at[region].shape, fill, jnp.float32)

    def halo_wait(ref, slot):
        for index, d in enumerate(DIRECTIONS):
            @pl.when(exists(d))
            def _():
                halo_copy(ref, slot, index, d).wait_send()

            back = tuple(-s for s in d)

            @pl.when(exists(back))
            def _():
                halo_copy(ref, slot, index, d).wait_recv()

    def sum_copies(slot, stage):
        count = counts[stage]
        copies = []
        for j in range(1, count):
            target = list(me)
            target[stage] = lax.rem(me[stage] + j, count)
            copies.append(
                pltpu.make_async_remote_copy(
                    src_ref=sums.at[slot, stage],
                    dst_ref=parts.at[slot, stage, me[stage]],
                    send_sem=sum_send.at[slot, stage, j],
                    recv_sem=sum_recv.at[slot, stage, j],
                    device_id=tuple(target),
                    device_id_type=pl.DeviceIdType.MESH,
                )
            )
        return copies

    def reduced(slot, value):
        for stage in (2, 1, 0):
            if counts[stage] == 1:
                continue
            sums[slot, stage] = value
            parts[slot, stage, me[stage]] = value
            copies = sum_copies(slot, stage)
            for copy in copies:
                copy.start()
            for copy in copies:
                copy.wait()
            value = parts[slot, stage, 0]
            for k in range(1, counts[stage]):
                value = value + parts[slot, stage, k]
        total = jnp.sum(value, axis=1, keepdims=True)
        norm, product = total[:4], total[4:]

        def both(x):
            return x + jnp.concatenate([x[2:4], x[0:2]], axis=0)

        return both(norm), both(product)

    inside = pl.ds(tile, tz * tile)
    for a in range(tx):
        for b in range(ty):
            param_pad[a + 1, b + 1, :, inside] = params_ref[a, b]
            rem_pad[a + 1, b + 1, :, inside] = rhs_ref[a, b]
    halo_start(param_pad, 0, 1.0)
    halo_start(rem_pad, 1, 0.0)

    def source_block(ap, bp, p, widths):
        start = pl.multiple_of(p * tile, tile)
        turned = param_pad[ap, bp, :, pl.ds(start, tile)].T
        for m in range(5):
            columns[m] = jnp.broadcast_to(turned[:, m : m + 1], (tile, tile))

        def visit(a, b):
            for c in widths:
                o = (ap - 1 - a, bp - 1 - b, p - 1 - c)
                code = 9 * (o[0] + 1) + 3 * (o[1] + 1) + (o[2] + 1)
                t = (a * ty + b) * tz + c
                listed = jnp.right_shift(bits_ref[t], code) & 1
                own = param_pad[
                    a + 1, b + 1, :, pl.ds(pl.multiple_of((c + 1) * tile, tile), tile)
                ]
                distance = None
                for m in range(3):
                    gap = columns[m] - (own[m : m + 1] - o[m].astype(jnp.float32))
                    distance = gap * gap if distance is None else distance + gap * gap
                listed = listed.astype(jnp.float32)
                coulomb = lax.rsqrt(distance + columns[3] * own[3:4]) * (coulomb_scale * listed)
                response = jnp.exp(-(distance / (columns[4] + own[4:5]))) * (
                    response_scale * listed
                )
                rows = pl.ds(pl.multiple_of(code * tile, tile), tile)
                store[t, rows, 0:tile] = coulomb.astype(jnp.bfloat16)
                store[t, rows, tile : 2 * tile] = response.astype(jnp.bfloat16)

        def over_a(a, carry):
            def over_b(b, inner_carry):
                visit(a, b)
                return inner_carry

            return lax.fori_loop(
                jnp.maximum(bp - 2, 0), jnp.minimum(bp, ty - 1) + 1, over_b, carry
            )

        lax.fori_loop(jnp.maximum(ap - 2, 0), jnp.minimum(ap, tx - 1) + 1, over_a, 0)

    def edge_sources(ap, bp, first, second, wide):
        def step(s, carry):
            p = first + s * (second - first)
            base = s * (tz - wide)
            source_block(ap, bp, p, [base + w for w in range(wide)])
            return carry

        lax.fori_loop(0, 2, step, 0)

    def middle_sources(ap, bp):
        def step(p, carry):
            source_block(ap, bp, p, [p - 2, p - 1, p])
            return carry

        lax.fori_loop(2, tz, step, 0)

    def own_rows(body):
        def over(q, carry):
            body(1 + q // ty, 1 + q % ty)
            return carry

        lax.fori_loop(0, tx * ty, over, 0)

    def build_own(ap, bp):
        middle_sources(ap, bp)
        edge_sources(ap, bp, 1, tz, 2)

    own_rows(build_own)

    same = lax.broadcasted_iota(jnp.int32, (tile, 2 * tile), 0) == (
        lax.broadcasted_iota(jnp.int32, (tile, 2 * tile), 1) % tile
    )

    def clear(t, carry):
        rows = pl.ds(13 * tile, tile)
        block = store[t, rows, :].astype(jnp.float32)
        store[t, rows, :] = jnp.where(same, 0.0, block).astype(jnp.bfloat16)
        return carry

    lax.fori_loop(0, tx * ty * tz, clear, 0)

    halo_wait(param_pad, 0)

    own_rows(lambda ap, bp: edge_sources(ap, bp, 0, tz + 1, 1))

    def ghost_row(q, carry):
        ap = q // (ty + 2)
        bp = q % (ty + 2)
        own = (ap >= 1) & (ap <= tx) & (bp >= 1) & (bp <= ty)

        @pl.when(jnp.logical_not(own))
        def _():
            middle_sources(ap, bp)
            edge_sources(ap, bp, 1, tz, 2)
            edge_sources(ap, bp, 0, tz + 1, 1)

        return carry

    lax.fori_loop(0, (tx + 2) * (ty + 2), ghost_row, 0)
    halo_wait(rem_pad, 1)

    charge_rows = lax.broadcasted_iota(jnp.int32, (4, tile), 0) < 2

    def operate(out, first):
        def split(q, carry):
            ap = q // (ty + 2)
            bp = q % (ty + 2)
            value = rem_pad[ap, bp]
            upper = value.astype(jnp.bfloat16).astype(jnp.float32)
            lower = value - upper
            ones = jnp.ones((8, value.shape[1]), jnp.float32)
            lhs[ap, bp] = jnp.concatenate([upper, lower, ones], axis=0).astype(jnp.bfloat16)
            return carry

        lax.fori_loop(0, (tx + 2) * (ty + 2), split, 0)

        def one(t, carry):
            norm, product = carry
            a = t // (ty * tz)
            b = t // tz % ty
            c = t % tz
            window = pl.ds(pl.multiple_of(c * tile, tile), 3 * tile)
            rows = jnp.concatenate(
                [lhs[a + i, b + j, :, window] for i in range(3) for j in range(3)], axis=1
            )
            got = jnp.dot(rows, store[t], preferred_element_type=jnp.float32)
            pair = got[0:4] + got[4:8]
            pair = jnp.where(charge_rows, pair[:, :tile], -pair[:, tile:])
            here = pl.ds(pl.multiple_of(c * tile, tile), tile)
            there = pl.ds(pl.multiple_of((c + 1) * tile, tile), tile)
            if first:
                row_sums = jnp.where(charge_rows, got[8:12, :tile], got[8:12, tile:])
                own = aux_ref[a, b, :, here]
                diag[a, b, :, here] = row_sums + jnp.where(charge_rows, own[0:1], own[1:2])
            vector = rem_pad[a + 1, b + 1, :, there]
            swapped = jnp.concatenate([vector[2:4], vector[0:2]], axis=0)
            link = aux_ref[a, b, 2:3, here]
            image = diag[a, b, :, here] * vector + pair + link * swapped
            out[a + 1, b + 1, :, there] = image
            return (norm + vector * vector, product + vector * image)

        zero = jnp.zeros((4, tile), jnp.float32)
        norm, product = lax.fori_loop(0, tx * ty * tz, one, (zero, zero), unroll=2)
        return jnp.concatenate([norm, product], axis=0)

    interior = (pl.ds(1, tx), pl.ds(1, ty), slice(None), inside)
    norm_now = step_size = None
    for iteration in range(ITERS):
        last = iteration + 1 == ITERS
        image = ghosts.at[iteration]
        partial = operate(image, iteration == 0)
        if not last:
            halo_start(image, 2 + iteration, 0.0)
        norm_next, product = reduced(iteration, partial)
        if not last:
            halo_wait(image, 2 + iteration)
        if iteration == 0:
            beta = None
            step_size = norm_next / product
        else:
            beta = norm_next / norm_now
            step_size = norm_next / (product - beta * norm_next / step_size)
        norm_now = norm_next
        for a in range(tx):
            for b in range(ty):
                along_dir = rem_pad[a + 1, b + 1, :, inside]
                if beta is not None:
                    along_dir = along_dir + beta * direction[a, b]
                direction[a, b] = along_dir
                moved = step_size * along_dir
                sol_ref[a, b] = moved if beta is None else sol_ref[a, b] + moved
        if last:
            for a in range(tx):
                for b in range(ty):
                    along = image[a + 1, b + 1, :, inside] + beta * along_pad[a + 1, b + 1, :, inside]
                    res_ref[a, b] = rem_pad[a + 1, b + 1, :, inside] - step_size * along
        else:
            for a in range(tx + 2):
                for b in range(ty + 2):
                    along = image[a, b]
                    if beta is not None:
                        along = along + beta * along_pad[a, b]
                    along_pad[a, b] = along
                    rem_pad[a, b] = rem_pad[a, b] - step_size * along


def on_device(counts, positions, shield, width, hardness, softness, coupling, pair_bits, right_side):
    tx, ty, tz, tile = hardness.shape
    blank = jnp.ones_like(width)

    def rows(fields):
        stacked = jnp.stack(fields, axis=2)
        return stacked.reshape(tx, ty, len(fields), tz * tile)

    params = rows([positions[0], positions[1], positions[2], shield, width, blank, blank, blank])
    aux = rows([hardness, softness, coupling, blank])
    rhs = rows([right_side[f] for f in range(4)])
    padded = (tx + 2, ty + 2)
    lanes = (tz + 2) * tile
    peers = max(counts)
    field = jax.ShapeDtypeStruct((tx, ty, 4, tz * tile), jnp.float32)
    vmem = pl.BlockSpec(memory_space=pltpu.VMEM)
    sol, res = pl.pallas_call(
        functools.partial(kernel, counts, (tx, ty, tz), tile),
        out_shape=(field, field),
        in_specs=[pl.BlockSpec(memory_space=pltpu.SMEM), vmem, vmem, vmem],
        out_specs=(vmem, vmem),
        scratch_shapes=[
            pltpu.VMEM((tx * ty * tz, 27 * tile, 2 * tile), jnp.bfloat16),
            pltpu.VMEM(padded + (8, lanes), jnp.float32),
            pltpu.VMEM(padded + (4, lanes), jnp.float32),
            pltpu.VMEM(padded + (4, lanes), jnp.float32),
            pltpu.VMEM((ITERS,) + padded + (4, lanes), jnp.float32),
            pltpu.VMEM(padded + (16, lanes), jnp.bfloat16),
            pltpu.VMEM((5, tile, tile), jnp.float32),
            pltpu.VMEM((tx, ty, 4, tz * tile), jnp.float32),
            pltpu.VMEM((tx, ty, 4, tz * tile), jnp.float32),
            pltpu.VMEM((ITERS, 3, 8, tile), jnp.float32),
            pltpu.VMEM((ITERS, 3, peers, 8, tile), jnp.float32),
            pltpu.SemaphoreType.DMA((ITERS + 1, 26)),
            pltpu.SemaphoreType.DMA((ITERS + 1, 26)),
            pltpu.SemaphoreType.DMA((ITERS, 3, peers)),
            pltpu.SemaphoreType.DMA((ITERS, 3, peers)),
        ],
        compiler_params=pltpu.CompilerParams(
            has_side_effects=True, vmem_limit_bytes=67043328
        ),
    )(pair_bits.reshape(-1), params, rhs, aux)

    def fields(x):
        return x.reshape(tx, ty, 4, tz, tile).transpose(2, 0, 1, 3, 4)

    return fields(sol), fields(res)


def solution(mesh):
    counts = tuple(mesh.shape[axis] for axis in AXES)
    tiles = P("gx", "gy", "gz", None)
    four = P(None, "gx", "gy", "gz", None)
    return jax.shard_map(
        functools.partial(on_device, counts),
        mesh=mesh,
        in_specs=(four, tiles, tiles, tiles, tiles, tiles, P("gx", "gy", "gz"), four),
        out_specs=(four, four),
        check_vma=False,
    )
```

time: 629 us -> 176 us (0.28)
  other arithmetic: 283 us -> 0.78 us
  Pallas kernels: 0 us -> 167 us
  blocking collectives: 135 us -> 0 us
  matrix products: 106 us -> 0 us
  starting transfers between devices: 65.2 us -> 0 us
  waiting for transfers between devices: 16.2 us -> 0 us
    pallas_call x0 -> x1, Pallas kernels: none -> 167 us  [on_device(): pl.pallas_call(functools.partial(kernel, counts, (tx, ty, tz), tile), out...]
    dynamic_update_slice x27 -> x0, other arithmetic: 141 us -> none  [build(): lax.dynamic_update_index_in_dim(store_response, response, offset_code, 0)]
    reduce_sum x38 -> x0, other arithmetic: 136 us -> none  [the longest x27 135 us: build(): row_response = row_response + jnp.sum(response.astype(jnp.float32), axis=2)]
    psum x3 -> x0, blocking collectives: 135 us -> none  [two_products(): lax.psum((inner_local(vector, vector), inner_local(vector, applied)), ('g...]
    dot_general x8 -> x0, matrix products: 106 us -> none  [the longest x4 53.5 us: operate(): jnp.einsum('otij,oftj->fti', store_coulomb, stacked[:, :4], preferred_ele...]
    ppermute x24 -> x0, starting transfers between devices: 65.2 us -> none  [the longest x12 49.7 us: extended(): lax.ppermute(lax.slice_in_dim(block, block.shape[dim] - width, None, axis...]
    ppermute x24 -> x0, waiting for transfers between devices: 16.2 us -> none  [the longest x12 14.9 us: extended(): lax.ppermute(lax.slice_in_dim(block, block.shape[dim] - width, None, axis...]
    slice x164 -> x2, local copies, waits for them, and re-layouts: 8.14 us -> 0.76 us  [the longest x1 0.76 us: on_device(): positions[2]]
  transfers between devices with their start and end apart: 24 -> 0, of which waited for: 16 -> 0; matrix products, arithmetic and copies ran while one was open for 0% -> 0% of each run, Pallas kernels for 0% -> 0%
where the time goes in v1:
time: 176 us; the launch traced here: 175 us
  Pallas kernels  167 us (95%)
  local copies, waits for them, and re-layouts  6.75 us (4%)
    pallas_call x1, Pallas kernels, on_device(): pl.pallas_call(functools.partial(kernel, counts, (tx, ty, tz), tile), out...  167 us

profile of v1, /device:TPU:0, one launch (start us, length us, event | category | flops | bytes accessed | tf_op | source)
XLA Modules:
  0.0 174.9 jit_solution(369887814934420146)
XLA Ops:
  0.6 0.0 copy-start.7
  0.6 0.7 copy-done.7
  1.3 0.7 reshape.43.bits_ref
  2.0 0.8 fusion.1
  2.7 0.0 copy-start.2
  2.7 0.0 copy-start.3
  2.8 0.7 copy-done.2
  3.5 0.0 copy-done.3
  3.5 0.0 copy-start
  3.5 0.8 stack.50.params_ref
  4.3 0.0 copy-done
  4.3 0.0 copy-start.4
  4.3 0.0 copy-start.5
  4.3 0.0 copy-start.6
  4.3 0.7 copy-done.4
  5.0 0.0 copy-done.5
  5.0 0.0 copy-done.6
  5.1 0.8 pad_maximum_fusion
  5.8 166.6 %shard_map.95 = (f32[2,2,4,1024]{3,2,1,0:T(4,128)}, f32[2,2,4,1024]{3,2,1,0:T(4,128)}) custom-call(s32[32]{0:T(128)} %reshape.43.bits_ref, f32[2,2,8,1024]{3,2,1,0:T(8,128)} %stack.50.params_ref, f32[2,2,4,1024]{3,2,1,0:T(4,128)} %get-tuple-element.13.rhs_ref, f32[2,2,4,1024]{3,2,1,0:T(4,128)} %get-tuple-element.14.aux_ref), custom_call_target="tpu_custom_call" | custom-call | tf_op jit(solution)/shard_map/pallas_call | solution.py:334
  172.5 0.9 reshape.44
  173.4 0.0 copy-start.1
  173.4 0.6 copy.15
  174.0 0.2 copy-done.1
  174.2 0.6 copy.14
  (4 shorter events, 0.1 us)
Async XLA Ops:
  0.6 0.7 copy-start.7
  2.7 0.7 copy-start.2
  2.7 0.7 copy-start.3
  3.5 0.8 copy-start
  4.3 0.7 copy-start.4
  4.3 0.7 copy-start.5
  4.3 0.7 copy-start.6
  173.4 0.8 copy-start.1

commit v2 on v1

--- a/solution.py
+++ b/solution.py
@@ -130,14 +130,33 @@
     halo_start(param_pad, 0, 1.0)
     halo_start(rem_pad, 1, 0.0)
 
+    row = lax.broadcasted_iota(jnp.int32, (8, tile), 0)
+
+    def centred(value):
+        return jnp.where(row < 3, value - 0.5, value)
+
+    def squares(value):
+        return value[0:1] * value[0:1] + value[1:2] * value[1:2] + value[2:3] * value[2:3]
+
+    def three(value):
+        first = value.astype(jnp.bfloat16).astype(jnp.float32)
+        rest = value - first
+        second = rest.astype(jnp.bfloat16).astype(jnp.float32)
+        return first, second, rest - second
+
     def source_block(ap, bp, p, widths):
         start = pl.multiple_of(p * tile, tile)
-        turned = param_pad[ap, bp, :, pl.ds(start, tile)].T
-        for m in range(5):
-            columns[m] = jnp.broadcast_to(turned[:, m : m + 1], (tile, tile))
-
-        def visit(a, b):
-            for c in widths:
+        raw = param_pad[ap, bp, :, pl.ds(start, tile)]
+        x = centred(raw)
+        x = jnp.where(row == 4, 0.0, jnp.where(row == 5, squares(x), x))
+        x = jnp.where(row == 7, 0.0, x)
+        x1, x2, x3 = three(x)
+        turned = jnp.concatenate([x1, x1, x1, x2, x2, x3, raw, raw], axis=0).T
+        columns[...] = jnp.broadcast_to(turned[:, 52:53], (tile, tile)) * -0.6931471805599453
+        partner = turned.astype(jnp.bfloat16)
+
+        def visit(rows_of_tiles):
+            for (a, b), c in itertools.product(rows_of_tiles, widths):
                 o = (ap - 1 - a, bp - 1 - b, p - 1 - c)
                 code = 9 * (o[0] + 1) + 3 * (o[1] + 1) + (o[2] + 1)
                 t = (a * ty + b) * tz + c
@@ -145,29 +164,43 @@
                 own = param_pad[
                     a + 1, b + 1, :, pl.ds(pl.multiple_of((c + 1) * tile, tile), tile)
                 ]
-                distance = None
-                for m in range(3):
-                    gap = columns[m] - (own[m : m + 1] - o[m].astype(jnp.float32))
-                    distance = gap * gap if distance is None else distance + gap * gap
+                shift = [step.astype(jnp.float32) for step in o]
+                shift = jnp.where(row == 0, shift[0], jnp.where(row == 1, shift[1], shift[2]))
+                r = centred(own) - shift
+                y = jnp.where(row < 3, -2.0 * r, jnp.where(row == 6, squares(r), own))
+                y = jnp.where((row == 4) | (row == 7), 0.0, y)
+                blank = jnp.zeros((16, tile), jnp.float32)
+                halves = []
+                for half in (jnp.where(row == 3, 0.0, y), y):
+                    y1, y2, y3 = three(half)
+                    halves.append(jnp.concatenate([y1, y2, y3, y1, y2, y1, blank], axis=0))
+                factors = jnp.concatenate(halves, axis=1).astype(jnp.bfloat16)
+                got = jnp.dot(partner, factors, preferred_element_type=jnp.float32)
                 listed = listed.astype(jnp.float32)
-                coulomb = lax.rsqrt(distance + columns[3] * own[3:4]) * (coulomb_scale * listed)
-                response = jnp.exp(-(distance / (columns[4] + own[4:5]))) * (
-                    response_scale * listed
-                )
+                coulomb = lax.rsqrt(got[:, tile:]) * (coulomb_scale * listed)
+                span = columns[...] + own[4:5] * -0.6931471805599453
+                response = jnp.exp2(got[:, :tile] / span) * (response_scale * listed)
                 rows = pl.ds(pl.multiple_of(code * tile, tile), tile)
                 store[t, rows, 0:tile] = coulomb.astype(jnp.bfloat16)
                 store[t, rows, tile : 2 * tile] = response.astype(jnp.bfloat16)
 
-        def over_a(a, carry):
-            def over_b(b, inner_carry):
-                visit(a, b)
-                return inner_carry
-
-            return lax.fori_loop(
-                jnp.maximum(bp - 2, 0), jnp.minimum(bp, ty - 1) + 1, over_b, carry
-            )
-
-        lax.fori_loop(jnp.maximum(ap - 2, 0), jnp.minimum(ap, tx - 1) + 1, over_a, 0)
+        a_low, b_low = jnp.maximum(ap - 2, 0), jnp.maximum(bp - 2, 0)
+        wide = jnp.minimum(bp, ty - 1) + 1 - b_low
+        total = (jnp.minimum(ap, tx - 1) + 1 - a_low) * wide
+
+        def place(n):
+            return a_low + n // wide, b_low + n % wide
+
+        def two(n, carry):
+            visit([place(2 * n), place(2 * n + 1)])
+            return carry
+
+        def single(n, carry):
+            visit([place(total - 1)])
+            return carry
+
+        lax.fori_loop(0, total // 2, two, 0)
+        lax.fori_loop(0, total % 2, single, 0)
 
     def edge_sources(ap, bp, first, second, wide):
         def step(s, carry):
@@ -218,12 +251,35 @@
         ap = q // (ty + 2)
         bp = q % (ty + 2)
         own = (ap >= 1) & (ap <= tx) & (bp >= 1) & (bp <= ty)
-
-        @pl.when(jnp.logical_not(own))
+        held = (ap + me[0] >= 1) & (ap + me[0] <= tx + counts[0] - 1)
+        held = held & (bp + me[1] >= 1) & (bp + me[1] <= ty + counts[1] - 1)
+
+        @pl.when(jnp.logical_not(own) & held)
         def _():
             middle_sources(ap, bp)
             edge_sources(ap, bp, 1, tz, 2)
             edge_sources(ap, bp, 0, tz + 1, 1)
+
+        @pl.when(jnp.logical_not(own) & jnp.logical_not(held))
+        def _():
+            def over_a(a, inner):
+                def over_b(b, innermost):
+                    code = 9 * (ap - a) + 3 * (bp - b)
+                    rows = pl.ds(pl.multiple_of(code * tile, tile), 3 * tile)
+
+                    def over_c(c, last):
+                        store[(a * ty + b) * tz + c, rows, :] = jnp.zeros(
+                            (3 * tile, 2 * tile), jnp.bfloat16
+                        )
+                        return last
+
+                    return lax.fori_loop(0, tz, over_c, innermost)
+
+                return lax.fori_loop(
+                    jnp.maximum(bp - 2, 0), jnp.minimum(bp, ty - 1) + 1, over_b, inner
+                )
+
+            lax.fori_loop(jnp.maximum(ap - 2, 0), jnp.minimum(ap, tx - 1) + 1, over_a, 0)
 
         return carry
 
@@ -343,7 +399,7 @@
             pltpu.VMEM(padded + (4, lanes), jnp.float32),
             pltpu.VMEM((ITERS,) + padded + (4, lanes), jnp.float32),
             pltpu.VMEM(padded + (16, lanes), jnp.bfloat16),
-            pltpu.VMEM((5, tile, tile), jnp.float32),
+            pltpu.VMEM((tile, tile), jnp.float32),
             pltpu.VMEM((tx, ty, 4, tz * tile), jnp.float32),
             pltpu.VMEM((tx, ty, 4, tz * tile), jnp.float32),
             pltpu.VMEM((ITERS, 3, 8, tile), jnp.float32),

time: 176 us -> 150 us (0.85)
  Pallas kernels: 167 us -> 141 us
    pallas_call x1, Pallas kernels: 167 us -> 141 us  [on_device(): pl.pallas_call(functools.partial(kernel, counts, (tx, ty, tz), tile), out...]
where the time goes in v2:
time: 150 us; the launch traced here: 149 us
  Pallas kernels  141 us (94%)
  local copies, waits for them, and re-layouts  6.75 us (4%)
    pallas_call x1, Pallas kernels, on_device(): pl.pallas_call(functools.partial(kernel, counts, (tx, ty, tz), tile), out...  141 us

profile of v2, /device:TPU:0, one launch (start us, length us, event | category | flops | bytes accessed | tf_op | source)
XLA Modules:
  0.0 148.9 jit_solution(16266380332680322883)
XLA Ops:
  0.6 0.0 copy-start.7
  0.6 0.7 copy-done.7
  1.3 0.7 reshape.43.bits_ref
  2.0 0.8 fusion.1
  2.7 0.0 copy-start.2
  2.7 0.0 copy-start.3
  2.8 0.7 copy-done.2
  3.5 0.0 copy-done.3
  3.5 0.0 copy-start
  3.5 0.8 stack.50.params_ref
  4.3 0.0 copy-done
  4.3 0.0 copy-start.4
  4.3 0.0 copy-start.5
  4.3 0.0 copy-start.6
  4.3 0.7 copy-done.4
  5.0 0.0 copy-done.5
  5.0 0.0 copy-done.6
  5.1 0.8 pad_maximum_fusion
  5.8 140.7 %shard_map.95 = (f32[2,2,4,1024]{3,2,1,0:T(4,128)}, f32[2,2,4,1024]{3,2,1,0:T(4,128)}) custom-call(s32[32]{0:T(128)} %reshape.43.bits_ref, f32[2,2,8,1024]{3,2,1,0:T(8,128)} %stack.50.params_ref, f32[2,2,4,1024]{3,2,1,0:T(4,128)} %get-tuple-element.13.rhs_ref, f32[2,2,4,1024]{3,2,1,0:T(4,128)} %get-tuple-element.14.aux_ref), custom_call_target="tpu_custom_call" | custom-call | tf_op jit(solution)/shard_map/pallas_call | solution.py:390
  146.6 0.9 reshape.44
  147.4 0.0 copy-start.1
  147.4 0.6 copy.15
  148.1 0.2 copy-done.1
  148.3 0.6 copy.14
  (4 shorter events, 0.1 us)
Async XLA Ops:
  0.6 0.7 copy-start.7
  2.7 0.7 copy-start.2
  2.7 0.7 copy-start.3
  3.5 0.8 copy-start
  4.3 0.7 copy-start.4
  4.3 0.7 copy-start.5
  4.3 0.7 copy-start.6
  147.4 0.8 copy-start.1

commit v3 on v2

--- a/solution.py
+++ b/solution.py
@@ -82,38 +82,28 @@
             def _():
                 halo_copy(ref, slot, index, d).wait_recv()
 
-    def sum_copies(slot, stage):
-        count = counts[stage]
-        copies = []
-        for j in range(1, count):
-            target = list(me)
-            target[stage] = lax.rem(me[stage] + j, count)
-            copies.append(
-                pltpu.make_async_remote_copy(
-                    src_ref=sums.at[slot, stage],
-                    dst_ref=parts.at[slot, stage, me[stage]],
-                    send_sem=sum_send.at[slot, stage, j],
-                    recv_sem=sum_recv.at[slot, stage, j],
-                    device_id=tuple(target),
-                    device_id_type=pl.DeviceIdType.MESH,
-                )
+    rank = (me[0] * counts[1] + me[1]) * counts[2] + me[2]
+    hops = [h for h in itertools.product(*map(range, counts)) if any(h)]
+
+    def reduced(slot, value):
+        sums[slot] = value
+        parts[slot, rank] = value
+        copies = [
+            pltpu.make_async_remote_copy(
+                src_ref=sums.at[slot],
+                dst_ref=parts.at[slot, rank],
+                send_sem=sum_send.at[slot, j],
+                recv_sem=sum_recv.at[slot, j],
+                device_id=tuple(lax.rem(m + h, n) for m, h, n in zip(me, hop, counts)),
+                device_id_type=pl.DeviceIdType.MESH,
             )
-        return copies
-
-    def reduced(slot, value):
-        for stage in (2, 1, 0):
-            if counts[stage] == 1:
-                continue
-            sums[slot, stage] = value
-            parts[slot, stage, me[stage]] = value
-            copies = sum_copies(slot, stage)
-            for copy in copies:
-                copy.start()
-            for copy in copies:
-                copy.wait()
-            value = parts[slot, stage, 0]
-            for k in range(1, counts[stage]):
-                value = value + parts[slot, stage, k]
+            for j, hop in enumerate(hops)
+        ]
+        for copy in copies:
+            copy.start()
+        for copy in copies:
+            copy.wait()
+        value = jnp.sum(parts[slot], axis=0)
         total = jnp.sum(value, axis=1, keepdims=True)
         norm, product = total[:4], total[4:]
 
@@ -384,7 +374,7 @@
     rhs = rows([right_side[f] for f in range(4)])
     padded = (tx + 2, ty + 2)
     lanes = (tz + 2) * tile
-    peers = max(counts)
+    peers = counts[0] * counts[1] * counts[2]
     field = jax.ShapeDtypeStruct((tx, ty, 4, tz * tile), jnp.float32)
     vmem = pl.BlockSpec(memory_space=pltpu.VMEM)
     sol, res = pl.pallas_call(
@@ -402,12 +392,12 @@
             pltpu.VMEM((tile, tile), jnp.float32),
             pltpu.VMEM((tx, ty, 4, tz * tile), jnp.float32),
             pltpu.VMEM((tx, ty, 4, tz * tile), jnp.float32),
-            pltpu.VMEM((ITERS, 3, 8, tile), jnp.float32),
-            pltpu.VMEM((ITERS, 3, peers, 8, tile), jnp.float32),
+            pltpu.VMEM((ITERS, 8, tile), jnp.float32),
+            pltpu.VMEM((ITERS, peers, 8, tile), jnp.float32),
             pltpu.SemaphoreType.DMA((ITERS + 1, 26)),
             pltpu.SemaphoreType.DMA((ITERS + 1, 26)),
-            pltpu.SemaphoreType.DMA((ITERS, 3, peers)),
-            pltpu.SemaphoreType.DMA((ITERS, 3, peers)),
+            pltpu.SemaphoreType.DMA((ITERS, peers)),
+            pltpu.SemaphoreType.DMA((ITERS, peers)),
         ],
         compiler_params=pltpu.CompilerParams(
             has_side_effects=True, vmem_limit_bytes=67043328

time: 150 us -> 143 us (0.953)
  Pallas kernels: 141 us -> 134 us
    pallas_call x1, Pallas kernels: 141 us -> 134 us  [on_device(): pl.pallas_call(functools.partial(kernel, counts, (tx, ty, tz), tile), out...]
where the time goes in v3:
time: 143 us; the launch traced here: 142 us
  Pallas kernels  134 us (94%)
  local copies, waits for them, and re-layouts  6.75 us (5%)
    pallas_call x1, Pallas kernels, on_device(): pl.pallas_call(functools.partial(kernel, counts, (tx, ty, tz), tile), out...  134 us

profile of v3, /device:TPU:0, one launch (start us, length us, event | category | flops | bytes accessed | tf_op | source)
XLA Modules:
  0.0 142.1 jit_solution(12224495634326813300)
XLA Ops:
  0.6 0.0 copy-start.7
  0.6 0.7 copy-done.7
  1.3 0.7 reshape.43.bits_ref
  2.0 0.8 fusion.1
  2.7 0.0 copy-start.2
  2.7 0.0 copy-start.3
  2.8 0.7 copy-done.2
  3.5 0.0 copy-done.3
  3.5 0.0 copy-start
  3.5 0.8 stack.50.params_ref
  4.3 0.0 copy-done
  4.3 0.0 copy-start.4
  4.3 0.0 copy-start.5
  4.3 0.0 copy-start.6
  4.3 0.7 copy-done.4
  5.0 0.0 copy-done.5
  5.0 0.0 copy-done.6
  5.1 0.8 pad_maximum_fusion
  5.8 133.8 %shard_map.95 = (f32[2,2,4,1024]{3,2,1,0:T(4,128)}, f32[2,2,4,1024]{3,2,1,0:T(4,128)}) custom-call(s32[32]{0:T(128)} %reshape.43.bits_ref, f32[2,2,8,1024]{3,2,1,0:T(8,128)} %stack.50.params_ref, f32[2,2,4,1024]{3,2,1,0:T(4,128)} %get-tuple-element.13.rhs_ref, f32[2,2,4,1024]{3,2,1,0:T(4,128)} %get-tuple-element.14.aux_ref), custom_call_target="tpu_custom_call" | custom-call | tf_op jit(solution)/shard_map/pallas_call | solution.py:380
  139.7 0.9 reshape.44
  140.5 0.0 copy-start.1
  140.6 0.6 copy.15
  141.2 0.2 copy-done.1
  141.4 0.6 copy.14
  (4 shorter events, 0.1 us)
Async XLA Ops:
  0.6 0.7 copy-start.7
  2.7 0.7 copy-start.2
  2.7 0.7 copy-start.3
  3.5 0.8 copy-start
  4.3 0.7 copy-start.4
  4.3 0.7 copy-start.5
  4.3 0.7 copy-start.6
  140.5 0.8 copy-start.1
